TPU v7x, 256 devices: a 8x8x2 block of a 8x8x16 slice. The times are simulated.
256 devices in a mesh: group: 2 (over z), seq: 128 (over y, x, core).
Axes of the slice: x: 8, y: 8, z: 2, core: 2. Of those that a mesh axis runs over, the one named last changes fastest.
The devices are a block of a 8x8x16 slice.
Arguments:
- tokens: bfloat16 [131072, 4096], P(('group', 'seq')), parts along dimension 0, may hold values from -6 to 6
- norm_gain: bfloat16 [4096], replicated, may hold values from 0.099609375 to 1.8984375
- w_key: bfloat16 [4096, 1024], P('seq'), may hold values from -0.09375 to 0.09375
- w_value: bfloat16 [4096, 1024], P('seq'), may hold values from -0.09375 to 0.09375
- lengths: int32 [4], P('group'), parts along dimension 0, may hold values from 16384 to 32768
- page_table: int32 [8192], P(('group', 'seq')), parts along dimension 0, may hold values from 0 to 5119, as said below
Outputs:
- kv_cache: bfloat16 [2, 10240, 16, 1024], P(None, ('group', 'seq')), parts along dimension 1
There are 2 independent parts, one for each index of `group`. A program takes and returns all parts, laid end to end along the dimension named above; an argument that names none is the same for every part. Nothing has to cross between parts.
Inputs may be any that keep to these rules, and one draw needn't show every extreme that they name: The entries are distinct. Page g of the 32 pages of device s goes to slot page_table[g] of decode device page_table[g] // 40, which is s + k modulo 128 for an offset k in -2 .. 2, at a slot of the block of 8 slots from (k + 2) * 8 on; so at most 8 pages go from one device to one decode device, and exactly 8 from every device to some decode device.
All inputs are finite; a program needn't handle non-finite values.
Results may differ from a plain program's by a relative error of at most 0.0049.
Values may be sent and summed in bfloat16 or wider, within the bound.
A program may use at most 64 MiB of HBM per device.

v0:
```python
import jax
import jax.numpy as jnp
from jax import lax
from jax.sharding import PartitionSpec as P

HEAD = 128
PAGE = 16
REACH = 2
CAP = 8
SLOTS = 40


ROPE_THETA = 500000.0
EPS = 1e-05


def shifted(block, axis, distance):
    devices = range(lax.axis_size(axis))
    route = [((i - distance) % len(devices), i) for i in devices]
    return lax.ppermute(block, axis, route)


def side_by_side(arrays, axis, dim, along):
    both = jnp.concatenate(arrays, axis=along)
    whole, at, finished = (lax.all_gather(both, axis, axis=dim, tiled=True), 0, [])
    for a in arrays:
        finished.append(lax.slice_in_dim(whole, at, at + a.shape[along], axis=along))
        at += a.shape[along]
    return tuple(finished)


def rotate_keys(key_rows, position):
    half = HEAD // 2
    freq = ROPE_THETA ** (-(jnp.arange(half, dtype=jnp.float32) * 2.0 / HEAD))
    angle = position.astype(jnp.float32)[:, None] * freq[None, :]
    cosine = jnp.cos(angle)[:, None, :]
    sine = jnp.sin(angle)[:, None, :]
    shaped = key_rows.reshape(key_rows.shape[0], -1, HEAD)
    first = shaped[:, :, :half]
    second = shaped[:, :, half:]
    turned = jnp.concatenate(
        [first * cosine - second * sine, second * cosine + first * sine], axis=2
    )
    return turned.reshape(key_rows.shape)


def hand_over(placed):
    regions = [
        placed[:, (offset + REACH) * CAP : (offset + REACH + 1) * CAP]
        for offset in range(-REACH, REACH + 1)
    ]
    pending = jnp.concatenate(regions[REACH + 1 :], axis=1)
    upward = []
    for step_index in range(REACH):
        moved = shifted(pending, "seq", 1)
        upward.append(moved[:, :CAP])
        pending = moved[:, CAP:]
    pending = jnp.concatenate(regions[:REACH][::-1], axis=1)
    downward = []
    for step_index in range(REACH):
        moved = shifted(pending, "seq", -1)
        downward.append(moved[:, :CAP])
        pending = moved[:, CAP:]
    arrived = downward[::-1] + [regions[REACH]] + upward
    return jnp.concatenate(arrived, axis=1)


def on_device(tokens, norm_gain, w_key, w_value, lengths, page_table):
    axis_size = lax.axis_size("seq")
    device_index = lax.axis_index("seq")
    tok_rows = tokens.shape[0]
    length_each = tok_rows * axis_size // 2
    token_index = device_index * tok_rows + jnp.arange(tok_rows, dtype=jnp.int32)
    prompt_id = token_index // length_each
    position = token_index % length_each
    limit = jnp.where(prompt_id == 0, lengths[0], lengths[1])
    inside = (position < limit)[:, None]
    wide = tokens.astype(jnp.float32)
    scale = lax.rsqrt(jnp.mean(wide * wide, axis=1, keepdims=True) + EPS)
    normed = (wide * scale * norm_gain.astype(jnp.float32)[None, :]).astype(jnp.bfloat16)
    page_count = tok_rows // PAGE
    local_slot = page_table % SLOTS
    slot_onehot = (jnp.arange(SLOTS, dtype=jnp.int32)[:, None] == local_slot[None, :]).astype(
        jnp.bfloat16
    )
    key_whole, value_whole = side_by_side((w_key, w_value), "seq", 0, 1)
    key_rows = jnp.dot(normed, key_whole, preferred_element_type=jnp.float32)
    value_rows = jnp.dot(normed, value_whole, preferred_element_type=jnp.float32)
    columns = key_rows.shape[1]
    keys = jnp.where(inside, rotate_keys(key_rows, position), 0.0).astype(jnp.bfloat16)
    values = jnp.where(inside, value_rows, 0.0).astype(jnp.bfloat16)
    stacked = jnp.stack([keys, values]).reshape(2, page_count, PAGE * columns)
    placed = jnp.einsum(
        "sp,cpx->csx", slot_onehot, stacked, preferred_element_type=jnp.float32
    ).astype(jnp.bfloat16)
    return hand_over(placed).reshape(2, SLOTS, PAGE, columns)


def solution(mesh):
    placed = (
        P(("group", "seq"), None),
        P(),
        P("seq", None),
        P("seq", None),
        P("group"),
        P(("group", "seq")),
    )
    return jax.shard_map(
        on_device,
        mesh=mesh,
        in_specs=placed,
        out_specs=P(None, ("group", "seq"), None, None),
        check_vma=False,
    )
```

profile of v0, /device:TPU:513, one launch (start us, length us, event | category | flops | bytes accessed | tf_op | source)
XLA Modules:
  0.0 199.9 jit_solution(16102729591982064031)
XLA Ops:
  6.5 0.0 all-gather.2.cloned.1.call-start
  6.6 1.5 pad_maximum_fusion.2
  8.1 0.1 all-gather.2.cloned.1.call-update
  8.1 0.7 convert_element_type.38
  8.8 1.4 fusion.29
  10.2 1.3 select_compare_fusion
  11.6 0.2 broadcast_in_dim.41
  11.8 1.3 broadcast_in_dim.42
  13.1 0.7 and_select_fusion
  13.8 3.1 %fusion.1 = f32[512]{0:T(512)S(1)} fusion(bf16[512,4096]{1,0:T(8,128)(2,1)} %param.6), kind=kLoop, calls=%fused_computation.4 | loop fusion | flops 6290944 | bytes 4196352 | tf_op jit(solution)/shard_map/reduce_sum | solution.py:79
  16.8 1.0 multiply_cosine_fusion
  17.8 108.1 %all-gather.2.cloned.1.call-done = bf16[4096,2048]{1,0:T(8,128)(2,1)} async-done(((bf16[32,2048]{1,0:T(8,128)(2,1)}), bf16[4096,2048]{1,0:T(8,128)(2,1)}) %all-gather.2.cloned.1.call-update) | async-done | bytes 16777232 | tf_op jit(solution)/shard_map/all_gather | solution.py:25
  126.0 9.2 %select_convert_fusion = bf16[512,1024]{1,0:T(8,128)(2,1)S(1)} fusion(bf16[4096,2048]{1,0:T(8,128)(2,1)} %all-gather.2.cloned.1.call-done, bf16[512,4096]{1,0:T(8,128)(2,1)} %param.6, f32[4096]{0:T(1024)S(1)} %convert_element_type.38, f32[512]{0:T(512)S(1)} %add_rsqrt_fusion, pred[512]{0:T(512)(128)(4,1)S(1)} %select_compare_fusion), kind=kOutput, calls=%fused_computation.15 | convolution fusion | flops 4304404480 | bytes 13650432 | tf_op jit(solution)/shard_map/dot_general | solution.py:88
  135.2 0.5 stack.7
  135.7 8.3 %fusion.11 = f32[64,8,8,128]{3,1,2,0:T(8,128)S(1)} fusion(bf16[4096,2048]{1,0:T(8,128)(2,1)} %all-gather.2.cloned.1.call-done, bf16[512,4096]{1,0:T(8,128)(2,1)} %param.6, f32[4096]{0:T(1024)S(1)} %convert_element_type.38, f32[512]{0:T(512)S(1)} %add_rsqrt_fusion), kind=kOutput, calls=%fused_computation.19 | convolution fusion | flops 4303355904 | bytes 14698496 | tf_op jit(solution)/shard_map/dot_general | solution.py:87
  144.0 0.5 copy.7
  144.5 0.9 multiply_subtract_fusion
  145.4 0.6 pad_maximum_fusion
  146.0 0.5 reshape.141
  146.5 1.4 select_convert_fusion.1
  147.8 1.0 fusion
  148.8 0.1 fusion.27
  148.9 0.1 pad_maximum_fusion.1
  148.9 0.5 collective-permute-start
  149.5 14.0 %collective-permute-done = bf16[2,16,16384]{2,1,0:T(8,128)(2,1)S(1)} collective-permute-done((bf16[2,16,16384]{2,1,0:T(8,128)(2,1)S(1)}, bf16[2,16,16384]{2,1,0:T(8,128)(2,1)S(1)}, u32[]{:S(2)}, u32[]{:S(2)}) %collective-permute-start) | collective-permute-done | bytes 1048608 | tf_op jit(solution)/shard_map/ppermute | solution.py:20
  163.5 1.9 collective-permute-start.1
  165.4 0.1 concatenate.21
  165.5 0.1 collective-permute-start.2
  165.6 6.6 %collective-permute-done.1 = bf16[2,8,16384]{2,1,0:T(8,128)(2,1)S(1)} collective-permute-done((bf16[2,8,16384]{2,1,0:T(8,128)(2,1)S(1)}, bf16[2,8,16384]{2,1,0:T(8,128)(2,1)S(1)}, u32[]{:S(2)}, u32[]{:S(2)}) %collective-permute-start.1) | collective-permute-done | bytes 524320 | tf_op jit(solution)/shard_map/ppermute | solution.py:20
  172.4 5.0 %collective-permute-done.2 = bf16[2,16,16384]{2,1,0:T(8,128)(2,1)S(1)} collective-permute-done((bf16[2,16,16384]{2,1,0:T(8,128)(2,1)S(1)}, bf16[2,16,16384]{2,1,0:T(8,128)(2,1)S(1)}, u32[]{:S(2)}, u32[]{:S(2)}) %collective-permute-start.2) | collective-permute-done | bytes 1048608 | tf_op jit(solution)/shard_map/ppermute | solution.py:20
  177.3 0.1 fusion.28
  177.4 2.6 %collective-permute-start.3 = (bf16[2,8,16384]{2,1,0:T(8,128)(2,1)S(1)}, bf16[2,8,16384]{2,1,0:T(8,128)(2,1)S(1)}, u32[]{:S(2)}, u32[]{:S(2)}) collective-permute-start(bf16[2,8,16384]{2,1,0:T(8,128)(2,1)S(1)} %get-tuple-element.9), channel_id=1, source_target_pairs={{127,0},{0,1},{1,2},{2,3},{3,4},{4,5},{5,6},{6,7},{7,8},{8,9},{9,1... | collective-permute-start | bytes 1572872 | tf_op jit(solution)/shard_map/ppermute | solution.py:20
  180.0 9.9 %collective-permute-done.3 = bf16[2,8,16384]{2,1,0:T(8,128)(2,1)S(1)} collective-permute-done((bf16[2,8,16384]{2,1,0:T(8,128)(2,1)S(1)}, bf16[2,8,16384]{2,1,0:T(8,128)(2,1)S(1)}, u32[]{:S(2)}, u32[]{:S(2)}) %collective-permute-start.3) | collective-permute-done | bytes 524320 | tf_op jit(solution)/shard_map/ppermute | solution.py:20
  190.0 3.1 %copy.8 = bf16[10,8,16,1024]{3,2,1,0:T(8,128)(2,1)} copy(bf16[10,8,16,1024]{3,1,2,0:T(8,128)(2,1)S(1)} %bitcast.17) | data formatting | bytes 5242880
  (8 shorter events, 0.2 us)
Async XLA Ops:
  6.5 119.4 %all-gather.2.cloned.1.call-start = ((), (), s32[]{:S(2)}) async-start(), calls=%async_computation | async-start | bytes 16908288 | tf_op jit(solution)/shard_map/all_gather | solution.py:25
  148.9 14.5 %collective-permute-start = (bf16[2,16,16384]{2,1,0:T(8,128)(2,1)S(1)}, bf16[2,16,16384]{2,1,0:T(8,128)(2,1)S(1)}, u32[]{:S(2)}, u32[]{:S(2)}) collective-permute-start(bf16[2,16,16384]{2,1,0:T(8,128)(2,1)S(1)} %pad_maximum_fusion.1), channel_id=1, source_target_pairs={{1,0},{2,1},{3,2},{4,3},{5,4},{6,5},{7,6},{8,7},{9,8},{10,9},{11,1... | collective-permute-start | bytes 3145736 | tf_op jit(solution)/shard_map/ppermute | solution.py:20
  163.5 8.7 %collective-permute-start.1 = (bf16[2,8,16384]{2,1,0:T(8,128)(2,1)S(1)}, bf16[2,8,16384]{2,1,0:T(8,128)(2,1)S(1)}, u32[]{:S(2)}, u32[]{:S(2)}) collective-permute-start(bf16[2,8,16384]{2,1,0:T(8,128)(2,1)S(1)} %slice.61), channel_id=1, source_target_pairs={{1,0},{2,1},{3,2},{4,3},{5,4},{6,5},{7,6},{8,7},{9,8},{10,9},{11,1... | collective-permute-start | bytes 1572872 | tf_op jit(solution)/shard_map/ppermute | solution.py:20
  165.5 11.9 %collective-permute-start.2 = (bf16[2,16,16384]{2,1,0:T(8,128)(2,1)S(1)}, bf16[2,16,16384]{2,1,0:T(8,128)(2,1)S(1)}, u32[]{:S(2)}, u32[]{:S(2)}) collective-permute-start(bf16[2,16,16384]{2,1,0:T(8,128)(2,1)S(1)} %concatenate.21), channel_id=1, source_target_pairs={{127,0},{0,1},{1,2},{2,3},{3,4},{4,5},{5,6},{6,7},{7,8},{8,9},{9,1... | collective-permute-start | bytes 3145736 | tf_op jit(solution)/shard_map/ppermute | solution.py:20
  177.4 12.5 %collective-permute-start.3 = (bf16[2,8,16384]{2,1,0:T(8,128)(2,1)S(1)}, bf16[2,8,16384]{2,1,0:T(8,128)(2,1)S(1)}, u32[]{:S(2)}, u32[]{:S(2)}) collective-permute-start(bf16[2,8,16384]{2,1,0:T(8,128)(2,1)S(1)} %get-tuple-element.9), channel_id=1, source_target_pairs={{127,0},{0,1},{1,2},{2,3},{3,4},{4,5},{5,6},{6,7},{7,8},{8,9},{9,1... | collective-permute-start | bytes 1572872 | tf_op jit(solution)/shard_map/ppermute | solution.py:20
Sparse Core Ops, SparseCore 0:
  9.9 115.9 all-gather.1
where the time goes:
time: 204 us; the launch traced here: 200 us
  waiting for transfers between devices  144 us (71%)
  matrix products  18.4 us (9%)
  between operations  13.6 us (7%)
  other arithmetic  11.2 us (5%)
  local copies, waits for them, and re-layouts  7.81 us (4%)
  starting transfers between devices  5.15 us (3%)
    all_gather x1, waiting for transfers between devices, side_by_side(): lax.all_gather(both, axis, axis=dim, tiled=True)  108 us
    ppermute x4, waiting for transfers between devices, shifted(): return lax.ppermute(block, axis, route)  35.5 us
    dot_general x1, matrix products, on_device(): jnp.dot(normed, value_whole, preferred_element_type=jnp.float32)  9.2 us
    dot_general x1, matrix products, on_device(): key_rows = jnp.dot(normed, key_whole, preferred_element_type=jnp.float32)  8.28 us
    ppermute x4, starting transfers between devices, shifted(): return lax.ppermute(block, axis, route)  5.15 us
  transfers between devices with their start and end apart: 5, of which 5 were waited for; matrix products, arithmetic and copies ran while one was open for 5% of the time, Pallas kernels for 0%

commit v1 on v0

v1 whole, which is shorter than its diff:
```python
import functools
import math

import jax
import jax.numpy as jnp
import numpy as np
from jax import lax
from jax.experimental import pallas as pl
from jax.experimental.pallas import tpu as pltpu
from jax.sharding import PartitionSpec as P

HEAD = 128
PAGE = 16
REACH = 2
CAP = 8
SLOTS = 40
PROMPTS = 2

ROPE_THETA = 500000.0
EPS = 1e-05

MESH = pl.DeviceIdType.MESH
CHUNKS = 4
FIRST = 32
SECOND = 16


def kernel(
    side,
    tokens_hbm,
    gain_ref,
    freq_ref,
    wk_hbm,
    wv_hbm,
    lengths_ref,
    table_ref,
    table_hbm,
    out,
    rows,
    weights,
    stage,
    total,
    cosine,
    sine,
    parcel,
    table_vec,
    table_smem,
    slot_vec,
    slot_smem,
    local_sem,
    swap_send,
    swap_recv,
    xs_send,
    xs_recv,
    ys_send,
    ys_recv,
    xb_send,
    xb_recv,
    yb_send,
    yb_recv,
    z_send,
    z_recv,
    page_send,
    page_recv,
):
    n_tok, depth = tokens_hbm.shape
    width = weights.shape[4]
    half_cols = width * (CHUNKS // 2)
    reach = side // 2
    half = side // 2
    block = weights.shape[3]

    group = lax.axis_index("group")
    me = lax.axis_index("seq")
    core = me % 2
    chip = me // 2
    x = chip % side
    y = chip // side
    chips = side * side
    parity = group % 2

    def device(yy, xx, cc):
        index = (((yy + side) % side) * side + (xx + side) % side) * 2 + cc
        return (group, index)

    partner = (group, chip * 2 + 1 - core)
    opposite = (group + 1 - 2 * parity, me)
    next_chip = (chip + 1) % chips
    prev_chip = (chip + chips - 1) % chips
    x_to = {1: device(y, x + 1, core), -1: device(y, x - 1, core)}
    y_to = {1: device(y + 1, x, core), -1: device(y - 1, x, core)}

    first_rows = pl.ds(0, FIRST)
    second_rows = pl.ds(pl.multiple_of(FIRST + SECOND * parity, SECOND), SECOND)
    other_rows = pl.ds(pl.multiple_of(FIRST + SECOND * (1 - parity), SECOND), SECOND)
    shard_second = pl.ds(pl.multiple_of(SECOND * parity, SECOND), SECOND)

    sent = []

    def remote(src, dst, send_sem, recv_sem, to):
        return pltpu.make_async_remote_copy(
            src_ref=src,
            dst_ref=dst,
            send_sem=send_sem,
            recv_sem=recv_sem,
            device_id=to,
            device_id_type=MESH,
        )

    token_parts = 4
    part = n_tok // token_parts

    def token_local(i):
        return pltpu.make_async_copy(
            tokens_hbm.at[pl.ds(i * part, part)],
            rows.at[pl.ds(pl.multiple_of(core * n_tok + i * part, part), part)],
            local_sem.at[i],
        )

    def token_swap(i):
        return remote(
            tokens_hbm.at[pl.ds(i * part, part)],
            rows.at[pl.ds(pl.multiple_of(core * n_tok + i * part, part), part)],
            swap_send.at[i],
            swap_recv.at[i],
            partner,
        )

    def token_arrival(i):
        there = rows.at[pl.ds(pl.multiple_of((1 - core) * n_tok + i * part, part), part)]
        return remote(there, there, swap_send.at[i], swap_recv.at[i], partner)

    def columns_of(q, cc):
        return pl.ds(pl.multiple_of(cc * half_cols + (q % 2) * width, 128), width)

    def shard(q):
        return wk_hbm if q < CHUNKS // 2 else wv_hbm

    def own_first(q):
        return pltpu.make_async_copy(
            shard(q).at[:, columns_of(q, core)],
            weights.at[q, y, x, first_rows, :],
            local_sem.at[token_parts + q],
        )

    def own_second(q):
        return pltpu.make_async_copy(
            shard(q).at[shard_second, columns_of(q, core)],
            weights.at[q, y, x, second_rows, :],
            local_sem.at[token_parts + q],
        )

    def staged(kv):
        source = (wk_hbm, wv_hbm)[kv]
        return pltpu.make_async_copy(
            source.at[:, pl.ds(pl.multiple_of((1 - core) * half_cols, 128), half_cols)],
            stage.at[kv],
            local_sem.at[token_parts + CHUNKS + kv],
        )

    def give_first(q):
        return remote(
            stage.at[q // 2, :, pl.ds((q % 2) * width, width)],
            weights.at[q, y, x, first_rows, :],
            swap_send.at[token_parts + q],
            swap_recv.at[token_parts + q],
            partner,
        )

    def give_second(q):
        return remote(
            stage.at[q // 2, shard_second, pl.ds((q % 2) * width, width)],
            weights.at[q, y, x, second_rows, :],
            swap_send.at[token_parts + q],
            swap_recv.at[token_parts + q],
            partner,
        )

    def give_table():
        i = token_parts + CHUNKS
        return remote(
            table_hbm, table_vec, swap_send.at[i], swap_recv.at[i], partner
        )

    for kv in range(2):
        staged(kv).start()

    @pl.when(core == 0)
    def _():
        for q in range(CHUNKS):
            own_first(q).start()

    @pl.when(core == 1)
    def _():
        for q in range(CHUNKS):
            own_second(q).start()

    for i in range(token_parts):
        token_local(i).start()

    barrier = pltpu.get_barrier_semaphore()
    friends = [x_to[1], x_to[-1], y_to[1], y_to[-1], partner, opposite]
    for other in (next_chip, prev_chip):
        for cc in range(2):
            friends.append((group, other * 2 + cc))
    for friend in friends:
        pl.semaphore_signal(barrier, inc=1, device_id=friend, device_id_type=MESH)
    pl.semaphore_wait(barrier, len(friends))

    for kv in range(2):
        staged(kv).wait()

    @pl.when(core == 0)
    def _():
        for q in range(CHUNKS):
            give_first(q).start()

    @pl.when(core == 1)
    def _():
        for q in range(CHUNKS):
            give_second(q).start()

    give_table().start()
    for i in range(token_parts):
        token_swap(i).start()

    parts = ((0, 1), (1, CHUNKS - 1))

    def x_short(g, s, d, origin, to):
        q0, nq = parts[g]
        piece = weights.at[pl.ds(q0, nq), y, (origin + 2 * side) % side, first_rows, :]
        return remote(piece, piece, xs_send.at[g, (1 - d) // 2, s - 1], xs_recv.at[g, (1 - d) // 2, s - 1], to)

    def y_short(g, s, d, origin, to):
        q0, nq = parts[g]
        piece = weights.at[pl.ds(q0, nq), (origin + 2 * side) % side, x, second_rows, :]
        return remote(piece, piece, ys_send.at[g, (1 - d) // 2, s - 1], ys_recv.at[g, (1 - d) // 2, s - 1], to)

    def short_runs(g, s, d):
        return s < reach or d == (1 if g == 0 else -1)

    def short_send(g, s):
        for d in (1, -1):
            if short_runs(g, s, d):
                x_short(g, s, d, x - d * (s - 1), x_to[d]).start()
                y_short(g, s, d, y - d * (s - 1), y_to[d]).start()

    def short_wait(g, s):
        for d in (1, -1):
            if short_runs(g, s, d):
                x_short(g, s, d, x - d * s, x_to[d]).wait_recv()
                y_short(g, s, d, y - d * s, y_to[d]).wait_recv()

    def short_done(g, s):
        for d in (1, -1):
            if short_runs(g, s, d):
                x_short(g, s, d, x - d * (s - 1), x_to[d]).wait_send()
                y_short(g, s, d, y - d * (s - 1), y_to[d]).wait_send()

    def block_ready(g):
        q0, nq = parts[g]

        @pl.when(core == 0)
        def _():
            for q in range(q0, q0 + nq):
                own_first(q).wait()
                give_second(q).wait_recv()

        @pl.when(core == 1)
        def _():
            for q in range(q0, q0 + nq):
                own_second(q).wait()
                give_first(q).wait_recv()

    def half_at(h):
        return pl.ds(h * half, half)

    def long_halves(s, d):
        if s < reach:
            return (0, 1)
        return (0,) if d == 1 else (1,)

    def long_index(s, h):
        return 2 * (s - 1) + (h if s < reach else 0)

    def y_long(q, s, h, d, origin, to):
        piece = weights.at[q, (origin + 2 * side) % side, half_at(h), first_rows, :]
        i = long_index(s, h)
        return remote(piece, piece, yb_send.at[q, (1 - d) // 2, i], yb_recv.at[q, (1 - d) // 2, i], to)

    def x_long(q, s, h, d, origin, to):
        piece = weights.at[q, half_at(h), (origin + 2 * side) % side, second_rows, :]
        i = long_index(s, h)
        return remote(piece, piece, xb_send.at[q, (1 - d) // 2, i], xb_recv.at[q, (1 - d) // 2, i], to)

    def long_send(q, s, h, d):
        y_long(q, s, h, d, y - d * (s - 1), y_to[d]).start()
        x_long(q, s, h, d, x - d * (s - 1), x_to[d]).start()

    def long_wait(q, s, h, d):
        y_long(q, s, h, d, y - d * s, y_to[d]).wait_recv()
        x_long(q, s, h, d, x - d * s, x_to[d]).wait_recv()

    def long_done(q, s, h, d):
        y_long(q, s, h, d, y - d * (s - 1), y_to[d]).wait_send()
        x_long(q, s, h, d, x - d * (s - 1), x_to[d]).wait_send()

    def across(q, i, origin, plane_rows):
        piece = weights.at[q, :, (origin + 2 * side) % side, plane_rows, :]
        return remote(piece, piece, z_send.at[q, i], z_recv.at[q, i], opposite)

    across_list = [(0, 0)]
    for s in range(1, reach):
        across_list += [(1 + 2 * (s - 1), s), (2 + 2 * (s - 1), -s)]
    across_list.append((side - 1, reach))

    def across_send(q, i):
        across(q, i, x - across_list[i][1], second_rows).start()

    prompt_size = n_tok * 2 * chips // PROMPTS
    base = (chip * 2 * n_tok) % prompt_size
    limit = lengths_ref[(chip * 2 * n_tok) // prompt_size]

    def normalise(start, count, step):
        def one(i, carry):
            at = pl.ds(pl.multiple_of(start + i * step, step), step)
            span = 512 if depth % 512 == 0 else 128
            squares = jnp.zeros((step, 128), jnp.float32)
            for lo in range(0, depth, 128):
                wide = rows[at, lo : lo + 128].astype(jnp.float32)
                squares += wide * wide
            mean = jnp.sum(squares, axis=1, keepdims=True) * (1.0 / depth)
            scale = lax.rsqrt(mean + EPS)
            for lo in range(0, depth, span):
                wide = rows[at, lo : lo + span].astype(jnp.float32)
                rows[at, lo : lo + span] = (
                    wide * scale * gain_ref[:, lo : lo + span].astype(jnp.float32)
                ).astype(jnp.bfloat16)
            return carry

        lax.fori_loop(0, count, one, 0)

    def tables():
        count = 32
        lane = lax.broadcasted_iota(jnp.int32, (count, HEAD), 1)
        step = lax.broadcasted_iota(jnp.int32, (count, HEAD), 0)

        def one(i, carry):
            angle = (base + i * count + step).astype(jnp.float32) * freq_ref[...]
            at = pl.ds(i * (count // PAGE), count // PAGE)
            cosine[at] = jnp.cos(angle).reshape(count // PAGE, PAGE, HEAD)
            turn = jnp.sin(angle)
            turn = jnp.where(lane < HEAD // 2, -turn, turn)
            sine[at] = turn.reshape(count // PAGE, PAGE, HEAD)
            return carry

        lax.fori_loop(0, 2 * n_tok // count, one, 0)

    pages = n_tok // PAGE

    def slot_table(owner, entry):
        lane = lax.broadcasted_iota(jnp.int32, (8, 128), 1)
        row = lax.broadcasted_iota(jnp.int32, (8, 128), 0)
        found = jnp.zeros((8, 128), jnp.int32)
        for p in range(pages):
            told = jnp.where(row == 0, p, limit)
            found = jnp.where(lane == lax.rem(entry(p), SLOTS), told, found)
        slot_vec[owner] = found

    def slot_copy():
        return pltpu.make_async_copy(
            slot_vec, slot_smem, local_sem.at[token_parts + CHUNKS + 3]
        )

    deep = side * block

    def multiply(q, k):
        w = weights[q, k].reshape(deep, width)
        step = 256 if (2 * n_tok) % 256 == 0 else 2 * n_tok
        at_k = pl.ds(pl.multiple_of(k * deep, 128), deep)

        def one(i, carry):
            at = pl.ds(pl.multiple_of(i * step, step), step)
            got = jnp.dot(rows[at, at_k], w, preferred_element_type=jnp.float32)
            got = got.reshape(step // PAGE, PAGE, width)
            at = pl.ds(i * (step // PAGE), step // PAGE)
            total[at] = jnp.where(k == 0, 0.0, total[at]) + got
            return carry

        lax.fori_loop(0, 2 * n_tok // step, one, 0)

    def page_rows(owner, slot, is_key):
        page = owner * pages + slot_smem[owner, 0, slot]
        end = slot_smem[owner, 1, slot]
        value = total[page]
        if is_key:
            cosines, sines = cosine[page], sine[page]
            turned = []
            for head in range(width // HEAD):
                a = value[:, head * HEAD : (head + 1) * HEAD]
                turned.append(a * cosines + pltpu.roll(a, HEAD // 2, 1) * sines)
            value = jnp.concatenate(turned, axis=1)
        position = base + page * PAGE + lax.broadcasted_iota(jnp.int32, value.shape, 0)
        return jnp.where(position < end, value, 0.0).astype(jnp.bfloat16)

    def out_columns(q, cc):
        return pl.ds(pl.multiple_of(cc * half_cols + (q % 2) * width, 128), width)

    def pages_out(q, is_key):
        kv = q // 2
        mine = out_columns(q, core)

        def one(j, carry):
            parcel[q, j] = page_rows(1, 3 * CAP + j, is_key)
            parcel[q, CAP + j] = page_rows(0, 4 * CAP + j, is_key)
            parcel[q, 2 * CAP + j] = page_rows(1, 4 * CAP + j, is_key)
            parcel[q, 3 * CAP + j] = page_rows(1, j, is_key)
            parcel[q, 4 * CAP + j] = page_rows(0, CAP + j, is_key)
            parcel[q, 5 * CAP + j] = page_rows(0, j, is_key)
            far = 1 - core
            parcel[q, 6 * CAP + j] = page_rows(1, (1 + far) * CAP + j, is_key)
            parcel[q, 7 * CAP + j] = page_rows(0, (2 + far) * CAP + j, is_key)
            near = (1 + core) * CAP + j
            out[kv, near, :, mine] = page_rows(1, near, is_key)
            near = (2 + core) * CAP + j
            out[kv, near, :, mine] = page_rows(0, near, is_key)
            return carry

        lax.fori_loop(0, CAP, one, 0)

    parcels = (
        (0, 2 * CAP, 3 * CAP, 1, 0),
        (2 * CAP, CAP, 4 * CAP, 1, 1),
        (3 * CAP, 2 * CAP, 0, -1, 1),
        (5 * CAP, CAP, 0, -1, 0),
    )

    def page_send_of(q, i):
        at, count, slot, where, cc = parcels[i]
        chip_to = next_chip if where == 1 else prev_chip
        return remote(
            parcel.at[q, pl.ds(at, count)],
            out.at[q // 2, pl.ds(slot, count), :, out_columns(q, core)],
            page_send.at[q, i],
            page_recv.at[q, (1 - where) // 2, core],
            (group, chip_to * 2 + cc),
        )

    def page_swap(q):
        slot = pl.multiple_of((2 - core) * CAP, CAP)
        return remote(
            parcel.at[q, pl.ds(6 * CAP, 2 * CAP)],
            out.at[q // 2, pl.ds(slot, 2 * CAP), :, out_columns(q, core)],
            page_send.at[q, 4],
            page_recv.at[q, 2, 0],
            partner,
        )

    def pages_send(q):
        for i in range(len(parcels)):
            page_send_of(q, i).start()
        page_swap(q).start()

    def pages_arrive(q, cc):
        for i, (at, count, slot, where, target) in enumerate(parcels):
            if target != cc:
                continue
            for sender in range(2):
                there = out.at[q // 2, pl.ds(slot, count), :, out_columns(q, sender)]
                remote(
                    there, there, page_send.at[q, i], page_recv.at[q, (1 - where) // 2, sender], partner
                ).wait_recv()
        there = out.at[q // 2, pl.ds((1 + cc) * CAP, 2 * CAP), :, out_columns(q, 1 - cc)]
        remote(there, there, page_send.at[q, 4], page_recv.at[q, 2, 0], partner).wait_recv()

    step = 32
    per_part = part // step

    block_ready(0)
    short_send(0, 1)
    block_ready(1)
    short_send(1, 1)
    jobs = [
        lambda: slot_table(core, lambda p: table_ref[0, p]),
        tables,
    ]
    for i in range(token_parts):

        def job(i=i):
            token_local(i).wait()
            normalise(core * n_tok + i * part, per_part, step)

        jobs.append(job)
    share = -(-len(jobs) // reach)
    for s in range(1, reach + 1):
        for job in jobs[(s - 1) * share : s * share]:
            job()
        for g in range(2):
            short_wait(g, s)
            if s < reach:
                short_send(g, s + 1)

    def advance(q, s, h):
        for d in (1, -1):
            if h in long_halves(s, d):
                if s > 1:
                    long_wait(q, s - 1, h, d)
                long_send(q, s, h, d)
            elif s > 1:
                long_wait(q, s - 1, h, d)
        if h == 1 and s > 1:
            across_send(q, 1 + 2 * (s - 2))
            across_send(q, 2 + 2 * (s - 2))

    def finish(q):
        for d in (1, -1):
            for h in long_halves(reach, d):
                long_wait(q, reach, h, d)
        across_send(q, side - 1)
        for i, (_, distance) in enumerate(across_list):
            across(q, i, x - distance, other_rows).wait_recv()

    def gather(q, work):
        across_send(q, 0)
        at = 0
        for s in range(1, reach + 1):
            for h in range(2):
                advance(q, s, h)
                if at < len(work):
                    work[at]()
                at += 1
        for left in work[at:]:
            left()
        finish(q)

    work = []
    for i in range(token_parts):

        def job(i=i):
            token_arrival(i).wait_recv()
            normalise((1 - core) * n_tok + i * part, per_part, step)

        work.append(job)

    def other_table():
        give_table().wait_recv()
        copy = pltpu.make_async_copy(
            table_vec, table_smem, local_sem.at[token_parts + CHUNKS + 2]
        )
        copy.start()
        copy.wait()
        slot_table(1 - core, lambda p: table_smem[0, p])
        copy = slot_copy()
        copy.start()
        copy.wait()

    work.append(other_table)
    gather(0, work)

    def multiply_some(q, some):
        def one(k, carry):
            multiply(q, k)
            return carry

        lax.fori_loop(some[0], some[1], one, 0)

    def hand_over(q, is_key):
        pages_out(q, is_key)
        pages_send(q)

    slots = 4
    for q in range(1, CHUNKS):
        work = []
        for i in range(slots):
            some = (i * side // slots, (i + 1) * side // slots)
            work.append(functools.partial(multiply_some, q - 1, some))
        work.append(functools.partial(hand_over, q - 1, q - 1 < CHUNKS // 2))
        gather(q, work)

    last = CHUNKS - 1
    multiply_some(last, (0, side))
    hand_over(last, last < CHUNKS // 2)

    for cc in range(2):

        @pl.when(core == cc)
        def _(cc=cc):
            for q in range(CHUNKS):
                if cc == 0:
                    give_first(q).wait_send()
                else:
                    give_second(q).wait_send()

    give_table().wait_send()
    for i in range(token_parts):
        token_swap(i).wait_send()
    for s in range(1, reach + 1):
        for g in range(2):
            short_done(g, s)

    def chunk_done(q, carry):
        for s in range(1, reach + 1):
            for d in (1, -1):
                for h in long_halves(s, d):
                    long_done(q, s, h, d)
        for i, (_, distance) in enumerate(across_list):
            across(q, i, x - distance, second_rows).wait_send()
        for i in range(len(parcels)):
            page_send_of(q, i).wait_send()
        page_swap(q).wait_send()
        return carry

    lax.fori_loop(0, CHUNKS, chunk_done, 0)
    for cc in range(2):

        @pl.when(core == cc)
        def _(cc=cc):
            def arrive(q, carry):
                pages_arrive(q, cc)
                return carry

            lax.fori_loop(0, CHUNKS, arrive, 0)


def on_device(tokens, norm_gain, w_key, w_value, lengths, page_table):
    n_seq = lax.axis_size("seq")
    side = math.isqrt(n_seq // 2)
    n_tok, depth = tokens.shape
    share, features = w_key.shape
    width = features // CHUNKS
    block = 2 * share
    pages = n_tok // PAGE
    assert 2 * side * side == n_seq and side % 2 == 0
    assert block == FIRST + 2 * SECOND and share == FIRST
    assert block * side * side == depth and width % HEAD == 0
    half = HEAD // 2
    freq = np.float32(ROPE_THETA) ** (-(np.arange(half, dtype=np.float32) * 2.0 / HEAD))
    freq = np.concatenate([freq, freq]).astype(np.float32)[None, :]
    reach = side // 2
    dma = pltpu.SemaphoreType.DMA
    vmem = pl.BlockSpec(memory_space=pltpu.VMEM)
    smem = pl.BlockSpec(memory_space=pltpu.SMEM)
    hbm = pl.BlockSpec(memory_space=pltpu.HBM)
    table = page_table.reshape(1, pages)
    long_sems = dma((CHUNKS, 2, 2 * reach - 1))
    return pl.pallas_call(
        functools.partial(kernel, side),
        out_shape=jax.ShapeDtypeStruct((2, SLOTS, PAGE, features), jnp.bfloat16),
        in_specs=[hbm, vmem, vmem, hbm, hbm, smem, smem, hbm],
        out_specs=vmem,
        scratch_shapes=[
            pltpu.VMEM((2 * n_tok, depth), jnp.bfloat16),
            pltpu.VMEM((CHUNKS, side, side, block, width), jnp.bfloat16),
            pltpu.VMEM((2, share, features // 2), jnp.bfloat16),
            pltpu.VMEM((2 * pages, PAGE, width), jnp.float32),
            pltpu.VMEM((2 * pages, PAGE, HEAD), jnp.float32),
            pltpu.VMEM((2 * pages, PAGE, HEAD), jnp.float32),
            pltpu.VMEM((CHUNKS, 8 * CAP, PAGE, width), jnp.bfloat16),
            pltpu.VMEM((1, pages), jnp.int32),
            pltpu.SMEM((1, pages), jnp.int32),
            pltpu.VMEM((2, 8, 128), jnp.int32),
            pltpu.SMEM((2, 8, 128), jnp.int32),
            dma((12,)),
            dma((9,)),
            dma((9,)),
            dma((2, 2, reach)),
            dma((2, 2, reach)),
            dma((2, 2, reach)),
            dma((2, 2, reach)),
            long_sems,
            long_sems,
            long_sems,
            long_sems,
            dma((CHUNKS, side)),
            dma((CHUNKS, side)),
            dma((CHUNKS, 5)),
            dma((CHUNKS, 3, 2)),
        ],
        compiler_params=pltpu.CompilerParams(
            collective_id=0,
            has_side_effects=True,
            vmem_limit_bytes=56 * 1024 * 1024,
        ),
    )(tokens, norm_gain[None, :], jnp.asarray(freq), w_key, w_value, lengths, table, table)


def solution(mesh):
    placed = (
        P(("group", "seq"), None),
        P(),
        P("seq", None),
        P("seq", None),
        P("group"),
        P(("group", "seq")),
    )
    return jax.shard_map(
        on_device,
        mesh=mesh,
        in_specs=placed,
        out_specs=P(None, ("group", "seq"), None, None),
        check_vma=False,
    )
```

time: 204 us -> 157 us (0.77); the launches traced: 200 us -> 157 us
  Pallas kernels: 0 us -> 152 us
  waiting for transfers between devices: 144 us -> 0 us
  matrix products: 18.4 us -> 0 us
  between operations: 13.6 us -> 0.01 us
  other arithmetic: 11.2 us -> 0 us
  starting transfers between devices: 5.15 us -> 0 us
  local copies, waits for them, and re-layouts: 7.81 us -> 4.98 us
    pallas_call x0 -> x1, Pallas kernels: none -> 152 us  [on_device(): pl.pallas_call(functools.partial(kernel, side), out_shape=jax.ShapeDtypeS...]
    all_gather x1 -> x0, waiting for transfers between devices: 108 us -> none  [side_by_side(): lax.all_gather(both, axis, axis=dim, tiled=True)]
    ppermute x4 -> x0, waiting for transfers between devices: 35.5 us -> none  [shifted(): return lax.ppermute(block, axis, route)]
    dot_general x3 -> x0, matrix products: 18.4 us -> none  [the longest x1 9.2 us: on_device(): jnp.dot(normed, value_whole, preferred_element_type=jnp.float32)]
    ppermute x4 -> x0, starting transfers between devices: 5.15 us -> none  [shifted(): return lax.ppermute(block, axis, route)]
    reduce_sum x1 -> x0, other arithmetic: 3.08 us -> none  [on_device(): scale = lax.rsqrt(jnp.mean(wide * wide, axis=1, keepdims=True) + EPS)]
    concatenate x3 -> x0, other arithmetic: 2.17 us -> none  [the longest x1 1.52 us: side_by_side(): both = jnp.concatenate(arrays, axis=along)]
    convert_element_type x3 -> x0, other arithmetic: 2.07 us -> none  [the longest x1 1.36 us: on_device(): jnp.where(inside, rotate_keys(key_rows, position), 0.0).astype(jnp.bfloat16)]
  transfers between devices with their start and end apart: 5 -> 0, of which waited for: 5 -> 0; matrix products, arithmetic and copies ran while one was open for 5% -> 0% of each run, Pallas kernels for 0% -> 0%
where the time goes in v1:
time: 157 us
  Pallas kernels  152 us (97%)
  local copies, waits for them, and re-layouts  4.98 us (3%)
    pallas_call x1, Pallas kernels, on_device(): pl.pallas_call(functools.partial(kernel, side), out_shape=jax.ShapeDtypeS...  152 us
    unnamed x1, local copies, waits for them, and re-layouts  3.67 us

profile of v1, /device:TPU:513, one launch (start us, length us, event | category | flops | bytes accessed | tf_op | source)
XLA Modules:
  0.0 156.7 jit_solution(13855240162544489264)
XLA Ops:
  0.0 1.3 broadcast_in_dim.3.gain_ref
  1.3 151.8 %shard_map.73 = bf16[2,40,16,1024]{3,2,1,0:T(8,128)(2,1)} custom-call(bf16[512,4096]{1,0:T(8,128)(2,1)} %tokens_hbm.1, bf16[1,4096]{1,0:T(2,128)(2,1)} %broadcast_in_dim.3.gain_ref, f32[1,128]{1,0:T(1,128)} %constant.2.clone.freq_ref, bf16[32,1024]{1,0:T(8,128)(2,1)} %wk_hbm.1, bf16[32,1024]{1,0:T(8,128)(2,1)} %wv_hbm.1, s32[2]{0:T(128)} %lengths_ref.1, ...), custom_call_target="tpu_custom_call" | custom-call | tf_op jit(solution)/shard_map/pallas_call | solution.py:646
  153.1 3.7 %copy.9 = bf16[2,40,16,1024]{3,2,1,0:T(8,128)(2,1)} copy(bf16[2,40,16,1024]{3,2,1,0:T(8,128)(2,1)} %shard_map.73) | data formatting | bytes 5242880

commit v2 on v1

--- a/solution.py
+++ b/solution.py
@@ -50,6 +50,10 @@
     local_sem,
     swap_send,
     swap_recv,
+    xd_send,
+    xd_recv,
+    yd_send,
+    yd_recv,
     xs_send,
     xs_recv,
     ys_send,
@@ -199,7 +203,9 @@
         token_local(i).start()
 
     barrier = pltpu.get_barrier_semaphore()
-    friends = [x_to[1], x_to[-1], y_to[1], y_to[-1], partner, opposite]
+    friends = [partner, opposite]
+    for k in range(1, side):
+        friends += [device(y, x + k, core), device(y + k, x, core)]
     for other in (next_chip, prev_chip):
         for cc in range(2):
             friends.append((group, other * 2 + cc))
@@ -224,53 +230,81 @@
     for i in range(token_parts):
         token_swap(i).start()
 
-    parts = ((0, 1), (1, CHUNKS - 1))
-
-    def x_short(g, s, d, origin, to):
-        q0, nq = parts[g]
-        piece = weights.at[pl.ds(q0, nq), y, (origin + 2 * side) % side, first_rows, :]
-        return remote(piece, piece, xs_send.at[g, (1 - d) // 2, s - 1], xs_recv.at[g, (1 - d) // 2, s - 1], to)
-
-    def y_short(g, s, d, origin, to):
-        q0, nq = parts[g]
-        piece = weights.at[pl.ds(q0, nq), (origin + 2 * side) % side, x, second_rows, :]
-        return remote(piece, piece, ys_send.at[g, (1 - d) // 2, s - 1], ys_recv.at[g, (1 - d) // 2, s - 1], to)
-
-    def short_runs(g, s, d):
-        return s < reach or d == (1 if g == 0 else -1)
-
-    def short_send(g, s):
-        for d in (1, -1):
-            if short_runs(g, s, d):
-                x_short(g, s, d, x - d * (s - 1), x_to[d]).start()
-                y_short(g, s, d, y - d * (s - 1), y_to[d]).start()
-
-    def short_wait(g, s):
-        for d in (1, -1):
-            if short_runs(g, s, d):
-                x_short(g, s, d, x - d * s, x_to[d]).wait_recv()
-                y_short(g, s, d, y - d * s, y_to[d]).wait_recv()
-
-    def short_done(g, s):
-        for d in (1, -1):
-            if short_runs(g, s, d):
-                x_short(g, s, d, x - d * (s - 1), x_to[d]).wait_send()
-                y_short(g, s, d, y - d * (s - 1), y_to[d]).wait_send()
-
-    def block_ready(g):
-        q0, nq = parts[g]
-
+    def x_direct(k, origin):
+        piece = weights.at[0, y, (origin + side) % side, first_rows, :]
+        return remote(piece, piece, xd_send.at[k - 1], xd_recv.at[k - 1], device(y, x + k, core))
+
+    def y_direct(k, origin):
+        piece = weights.at[0, (origin + side) % side, x, second_rows, :]
+        return remote(piece, piece, yd_send.at[k - 1], yd_recv.at[k - 1], device(y + k, x, core))
+
+    near_first = sorted(range(1, side), key=lambda k: min(k, side - k))
+
+    def direct_wait():
+        for k in near_first:
+            x_direct(k, x - k).wait_recv()
+            y_direct(k, y - k).wait_recv()
+
+    later = pl.ds(1, CHUNKS - 1)
+
+    def x_short(s, d, origin, to):
+        piece = weights.at[later, y, (origin + 2 * side) % side, first_rows, :]
+        i = (1 - d) // 2
+        return remote(piece, piece, xs_send.at[i, s - 1], xs_recv.at[i, s - 1], to)
+
+    def y_short(s, d, origin, to):
+        piece = weights.at[later, (origin + 2 * side) % side, x, second_rows, :]
+        i = (1 - d) // 2
+        return remote(piece, piece, ys_send.at[i, s - 1], ys_recv.at[i, s - 1], to)
+
+    def short_ways(s):
+        return (1, -1) if s < reach else (-1,)
+
+    def short_send(s):
+        for d in short_ways(s):
+            x_short(s, d, x - d * (s - 1), x_to[d]).start()
+            y_short(s, d, y - d * (s - 1), y_to[d]).start()
+
+    def short_wait(s):
+        for d in short_ways(s):
+            x_short(s, d, x - d * s, x_to[d]).wait_recv()
+            y_short(s, d, y - d * s, y_to[d]).wait_recv()
+
+    def short_done(s):
+        for d in short_ways(s):
+            x_short(s, d, x - d * (s - 1), x_to[d]).wait_send()
+            y_short(s, d, y - d * (s - 1), y_to[d]).wait_send()
+
+    def x_begin():
+        for k in near_first:
+            x_direct(k, x).start()
+        for d in short_ways(1):
+            x_short(1, d, x, x_to[d]).start()
+
+    def y_begin():
+        for k in near_first:
+            y_direct(k, y).start()
+        for d in short_ways(1):
+            y_short(1, d, y, y_to[d]).start()
+
+    def begin():
         @pl.when(core == 0)
         def _():
-            for q in range(q0, q0 + nq):
+            for q in range(CHUNKS):
                 own_first(q).wait()
+            x_begin()
+            for q in range(CHUNKS):
                 give_second(q).wait_recv()
+            y_begin()
 
         @pl.when(core == 1)
         def _():
-            for q in range(q0, q0 + nq):
+            for q in range(CHUNKS):
                 own_second(q).wait()
+            y_begin()
+            for q in range(CHUNKS):
                 give_first(q).wait_recv()
+            x_begin()
 
     def half_at(h):
         return pl.ds(h * half, half)
@@ -476,38 +510,46 @@
     step = 32
     per_part = part // step
 
-    block_ready(0)
-    short_send(0, 1)
-    block_ready(1)
-    short_send(1, 1)
-    jobs = [
-        lambda: slot_table(core, lambda p: table_ref[0, p]),
-        tables,
-    ]
-    for i in range(token_parts):
-
-        def job(i=i):
-            token_local(i).wait()
-            normalise(core * n_tok + i * part, per_part, step)
-
-        jobs.append(job)
-    share = -(-len(jobs) // reach)
-    for s in range(1, reach + 1):
-        for job in jobs[(s - 1) * share : s * share]:
-            job()
-        for g in range(2):
-            short_wait(g, s)
-            if s < reach:
-                short_send(g, s + 1)
+    def own_rows(i):
+        token_local(i).wait()
+        normalise(core * n_tok + i * part, per_part, step)
+
+    def other_rows_in(i):
+        token_arrival(i).wait_recv()
+        normalise((1 - core) * n_tok + i * part, per_part, step)
+
+    def slot_tables():
+        give_table().wait_recv()
+        copy = pltpu.make_async_copy(
+            table_vec, table_smem, local_sem.at[token_parts + CHUNKS + 2]
+        )
+        copy.start()
+        slot_table(core, lambda p: table_ref[0, p])
+        copy.wait()
+        slot_table(1 - core, lambda p: table_smem[0, p])
+        slot_copy().start()
+
+    def multiply_some(q, some):
+        def one(k, carry):
+            multiply(q, k)
+            return carry
+
+        lax.fori_loop(some[0], some[1], one, 0)
+
+    def hand_over(q, is_key):
+        pages_out(q, is_key)
+        pages_send(q)
+
+    lag = 2
 
     def advance(q, s, h):
         for d in (1, -1):
+            if s > 1:
+                long_wait(q, s - 1, h, d)
             if h in long_halves(s, d):
-                if s > 1:
-                    long_wait(q, s - 1, h, d)
                 long_send(q, s, h, d)
-            elif s > 1:
-                long_wait(q, s - 1, h, d)
+        if s == 1 and h == 1:
+            across_send(q, 0)
         if h == 1 and s > 1:
             across_send(q, 1 + 2 * (s - 2))
             across_send(q, 2 + 2 * (s - 2))
@@ -517,69 +559,54 @@
             for h in long_halves(reach, d):
                 long_wait(q, reach, h, d)
         across_send(q, side - 1)
+
+    def across_wait(q):
         for i, (_, distance) in enumerate(across_list):
             across(q, i, x - distance, other_rows).wait_recv()
 
-    def gather(q, work):
-        across_send(q, 0)
-        at = 0
-        for s in range(1, reach + 1):
-            for h in range(2):
+    def pump(t, h):
+        for q in range(CHUNKS):
+            s = t - lag * q + 1
+            if 1 <= s <= reach:
                 advance(q, s, h)
-                if at < len(work):
-                    work[at]()
-                at += 1
-        for left in work[at:]:
-            left()
-        finish(q)
-
-    work = []
+            elif s == reach + 1 and h == 0:
+                finish(q)
+
+    points = {}
+
+    def at(t, h, job):
+        points.setdefault((t, h), []).append(job)
+
     for i in range(token_parts):
-
-        def job(i=i):
-            token_arrival(i).wait_recv()
-            normalise((1 - core) * n_tok + i * part, per_part, step)
-
-        work.append(job)
-
-    def other_table():
-        give_table().wait_recv()
-        copy = pltpu.make_async_copy(
-            table_vec, table_smem, local_sem.at[token_parts + CHUNKS + 2]
-        )
-        copy.start()
-        copy.wait()
-        slot_table(1 - core, lambda p: table_smem[0, p])
-        copy = slot_copy()
-        copy.start()
-        copy.wait()
-
-    work.append(other_table)
-    gather(0, work)
-
-    def multiply_some(q, some):
-        def one(k, carry):
-            multiply(q, k)
-            return carry
-
-        lax.fori_loop(some[0], some[1], one, 0)
-
-    def hand_over(q, is_key):
-        pages_out(q, is_key)
-        pages_send(q)
-
-    slots = 4
-    for q in range(1, CHUNKS):
-        work = []
-        for i in range(slots):
-            some = (i * side // slots, (i + 1) * side // slots)
-            work.append(functools.partial(multiply_some, q - 1, some))
-        work.append(functools.partial(hand_over, q - 1, q - 1 < CHUNKS // 2))
-        gather(q, work)
-
-    last = CHUNKS - 1
-    multiply_some(last, (0, side))
-    hand_over(last, last < CHUNKS // 2)
+        at(i // 2, i % 2, functools.partial(own_rows, i))
+        at(2 + i // 2, i % 2, functools.partial(other_rows_in, i))
+    at(2, 1, slot_tables)
+    for q in range(CHUNKS):
+        t = lag * q + reach
+        at(t, 1, functools.partial(across_wait, q))
+        at(t, 1, functools.partial(multiply_some, q, (0, side // 2)))
+        at(t + 1, 0, functools.partial(multiply_some, q, (side // 2, side)))
+        if q == 0:
+            at(t + 1, 0, lambda: slot_copy().wait())
+        at(t + 1, 1, functools.partial(hand_over, q, q < CHUNKS // 2))
+
+    begin()
+    tables()
+    short_wait(1)
+    if reach > 1:
+        short_send(2)
+    direct_wait()
+    for t in range(lag * (CHUNKS - 1) + reach + 2):
+        for h in range(2):
+            pump(t, h)
+            s = 2 * t + h + 2
+            if t < 2 and s <= reach:
+                short_wait(s)
+                if s < reach:
+                    short_send(s + 1)
+            for job in points.pop((t, h), ()):
+                job()
+    assert not points
 
     for cc in range(2):
 
@@ -595,8 +622,10 @@
     for i in range(token_parts):
         token_swap(i).wait_send()
     for s in range(1, reach + 1):
-        for g in range(2):
-            short_done(g, s)
+        short_done(s)
+    for k in near_first:
+        x_direct(k, x).wait_send()
+        y_direct(k, y).wait_send()
 
     def chunk_done(q, carry):
         for s in range(1, reach + 1):
@@ -663,10 +692,14 @@
             dma((12,)),
             dma((9,)),
             dma((9,)),
-            dma((2, 2, reach)),
-            dma((2, 2, reach)),
-            dma((2, 2, reach)),
-            dma((2, 2, reach)),
+            dma((side - 1,)),
+            dma((side - 1,)),
+            dma((side - 1,)),
+            dma((side - 1,)),
+            dma((2, reach)),
+            dma((2, reach)),
+            dma((2, reach)),
+            dma((2, reach)),
             long_sems,
             long_sems,
             long_sems,

time: 157 us -> 134 us (0.85)
  Pallas kernels: 152 us -> 129 us
    pallas_call x1, Pallas kernels: 152 us -> 129 us  [on_device(): pl.pallas_call(functools.partial(kernel, side), out_shape=jax.ShapeDtypeS...]
where the time goes in v2:
time: 134 us
  Pallas kernels  129 us (96%)
  local copies, waits for them, and re-layouts  4.98 us (4%)
    pallas_call x1, Pallas kernels, on_device(): pl.pallas_call(functools.partial(kernel, side), out_shape=jax.ShapeDtypeS...  129 us
    unnamed x1, local copies, waits for them, and re-layouts  3.67 us

profile of v2, /device:TPU:513, one launch (start us, length us, event | category | flops | bytes accessed | tf_op | source)
XLA Modules:
  0.0 133.9 jit_solution(1494194067366107097)
XLA Ops:
  0.0 1.3 broadcast_in_dim.3.gain_ref
  1.3 128.9 %shard_map.73 = bf16[2,40,16,1024]{3,2,1,0:T(8,128)(2,1)} custom-call(bf16[512,4096]{1,0:T(8,128)(2,1)} %tokens_hbm.1, bf16[1,4096]{1,0:T(2,128)(2,1)} %broadcast_in_dim.3.gain_ref, f32[1,128]{1,0:T(1,128)} %constant.2.clone.freq_ref, bf16[32,1024]{1,0:T(8,128)(2,1)} %wk_hbm.1, bf16[32,1024]{1,0:T(8,128)(2,1)} %wv_hbm.1, s32[2]{0:T(128)} %lengths_ref.1, ...), custom_call_target="tpu_custom_call" | custom-call | tf_op jit(solution)/shard_map/pallas_call | solution.py:675
  130.3 3.7 %copy.9 = bf16[2,40,16,1024]{3,2,1,0:T(8,128)(2,1)} copy(bf16[2,40,16,1024]{3,2,1,0:T(8,128)(2,1)} %shard_map.73) | data formatting | bytes 5242880
